TPU v7x, 32 devices: a whole 2x2x4 slice. The times are simulated.
32 devices in a mesh: gx: 8 (over y, x, core), gy: 4 (over z).
Axes of the slice: x: 2, y: 2, z: 4, core: 2. Of those that a mesh axis runs over, the one named last changes fastest.
Arguments:
- terminal: float32 [128, 2048], P('gx', 'gy'), may hold values from -15 to 15
- initial_density: float32 [128, 2048], P('gx', 'gy'), may hold values from 0.1 to 1
- density_guess: float32 [2, 128, 2048], P(None, 'gx', 'gy'), may hold values from 0.1 to 1
- diagonal: float32 [128, 2048], P('gx', 'gy'), may hold values from 0.1 to 2
Outputs:
- value_field: float32 [128, 2048], P('gx', 'gy')
- density_field: float32 [128, 2048], P('gx', 'gy')
All inputs are finite; a program needn't handle non-finite values.
Results may differ from a plain program's by a relative error of at most 0.00011.
Values sent between devices are 32-bit elements; how exact they have to be, the bound alone decides.
A program may use at most 64 MiB of HBM per device.

v0:
```python
import jax
import jax.numpy as jnp
from jax import lax
from jax.sharding import PartitionSpec as P

LEVELS = 2
STEPS = 3


inv_step = 0.5
coupling = 0.5


def padded_2(cells, sides, width):
    for axis, dim in sides:
        count = lax.axis_size(axis)
        ends = count - 1
        head = lax.slice_in_dim(cells, 0, width, axis=dim)
        tail = lax.slice_in_dim(cells, cells.shape[dim] - width, cells.shape[dim], axis=dim)
        cells = jnp.concatenate(
            [
                lax.ppermute(tail, axis, [(i, (i + 1) % count) for i in range(ends)]),
                cells,
                lax.ppermute(head, axis, [((i + 1) % count, i) for i in range(ends)]),
            ],
            axis=dim,
        )
    return cells


def apply_padded(padded, center, diagonal):
    beside = padded[2:, 1:-1] + padded[:-2, 1:-1] + padded[1:-1, 2:] + padded[1:-1, :-2]
    return (inv_step + diagonal) * center + (4.0 * center - beside)


def hamiltonian(padded):
    center = padded[1:-1, 1:-1]
    back_x = center - padded[:-2, 1:-1]
    ahead_x = padded[2:, 1:-1] - center
    back_y = center - padded[1:-1, :-2]
    ahead_y = padded[1:-1, 2:] - center
    return 0.5 * (
        jnp.maximum(back_x, 0.0) ** 2
        + jnp.minimum(ahead_x, 0.0) ** 2
        + jnp.maximum(back_y, 0.0) ** 2
        + jnp.minimum(ahead_y, 0.0) ** 2
    )


def divergence(pad_m, pad_u):
    m_mid = pad_m[1:-1, 1:-1]
    u_mid = pad_u[1:-1, 1:-1]
    speed_ahead = -(pad_u[2:, 1:-1] - u_mid)
    speed_back = -(u_mid - pad_u[:-2, 1:-1])
    flux_ahead = (
        jnp.maximum(speed_ahead, 0.0) * m_mid + jnp.minimum(speed_ahead, 0.0) * pad_m[2:, 1:-1]
    )
    flux_back = (
        jnp.maximum(speed_back, 0.0) * pad_m[:-2, 1:-1] + jnp.minimum(speed_back, 0.0) * m_mid
    )
    total = flux_ahead - flux_back
    speed_ahead = -(pad_u[1:-1, 2:] - u_mid)
    speed_back = -(u_mid - pad_u[1:-1, :-2])
    flux_ahead = (
        jnp.maximum(speed_ahead, 0.0) * m_mid + jnp.minimum(speed_ahead, 0.0) * pad_m[1:-1, 2:]
    )
    flux_back = (
        jnp.maximum(speed_back, 0.0) * pad_m[1:-1, :-2] + jnp.minimum(speed_back, 0.0) * m_mid
    )
    return total + flux_ahead - flux_back


def stencil(field, diagonal):
    padded = padded_2(field, (("gx", 0), ("gy", 1)), 1)
    return apply_padded(padded, field, diagonal)


def paired(resid, image):
    return lax.psum((jnp.sum(resid * resid), jnp.sum(resid * image)), ("gx", "gy"))


def solve(rhs, diagonal):
    answer = jnp.zeros_like(rhs)
    resid = rhs
    image = stencil(resid, diagonal)
    norm_now, product = paired(resid, image)
    alpha = norm_now / product
    direction = resid
    along = image
    for step in range(STEPS):
        answer = answer + alpha * direction
        if step + 1 < STEPS:
            resid = resid - alpha * along
            image = stencil(resid, diagonal)
            norm_next, product = paired(resid, image)
            ratio = norm_next / norm_now
            alpha = norm_next / (product - ratio * norm_next / alpha)
            direction = resid + ratio * direction
            along = image + ratio * along
            norm_now = norm_next
    return answer


def shards(terminal, initial_density, density_guess, diagonal):
    levels = [None] * LEVELS
    kept = [None] * (LEVELS + 1)
    later = terminal
    for level in reversed(range(LEVELS)):
        padded = padded_2(later, (("gx", 0), ("gy", 1)), 1)
        kept[level + 1] = padded
        rhs = inv_step * later - hamiltonian(padded) + coupling * density_guess[level]
        later = solve(rhs, diagonal)
        levels[level] = later
    density = initial_density
    for level in range(LEVELS):
        both = padded_2(jnp.stack([density, levels[level]]), (("gx", 1), ("gy", 2)), 1)
        pad_m = both[0]
        pad_u = both[1]
        rhs = inv_step * density - divergence(pad_m, pad_u)
        density = solve(rhs, diagonal)
    return (levels[0], density)


def solution(mesh):
    placed = (P("gx", "gy"), P("gx", "gy"), P(None, "gx", "gy"), P("gx", "gy"))
    return jax.shard_map(
        shards,
        mesh=mesh,
        in_specs=placed,
        out_specs=(P("gx", "gy"), P("gx", "gy")),
        check_vma=False,
    )
```

profile of v0, /device:TPU:0, one launch (start us, length us, event | category | flops | bytes accessed | tf_op | source)
XLA Modules:
  0.0 794.6 jit_solution(6539389510848766580)
XLA Ops:
  27.9 4.5 collective-permute-start.7
  34.6 42.7 %all-reduce.11 = (f32[]{:T(128)}, f32[]{:T(128)}) all-reduce(f32[]{:T(128)} %get-tuple-element.25, f32[]{:T(128)} %get-tuple-element.24), channel_id=1, replica_groups=mesh['gx'=8,'gy'=4] {'gx','gy'}, use_global_device_ids=true, to_apply=%region_1.0 | all-reduce | flops 2 | bytes 16 | tf_op jit(solution)/shard_map/psum | solution.py:79
  86.9 4.5 collective-permute-start.11
  93.6 42.6 %all-reduce.10 = (f32[]{:T(128)}, f32[]{:T(128)}) all-reduce(f32[]{:T(128)} %get-tuple-element.23, f32[]{:T(128)} %get-tuple-element.22), channel_id=1, replica_groups=mesh['gx'=8,'gy'=4] {'gx','gy'}, use_global_device_ids=true, to_apply=%region_5.0 | all-reduce | flops 2 | bytes 16 | tf_op jit(solution)/shard_map/psum | solution.py:79
  149.1 4.5 collective-permute-start.15
  155.8 41.8 %all-reduce.9 = (f32[]{:T(128)}, f32[]{:T(128)}) all-reduce(f32[]{:T(128)} %get-tuple-element.21, f32[]{:T(128)} %get-tuple-element.20), channel_id=1, replica_groups=mesh['gx'=8,'gy'=4] {'gx','gy'}, use_global_device_ids=true, to_apply=%region_9.0 | all-reduce | flops 2 | bytes 16 | tf_op jit(solution)/shard_map/psum | solution.py:79
  225.6 4.5 collective-permute-start.23
  232.2 42.6 %all-reduce.8 = (f32[]{:T(128)}, f32[]{:T(128)}) all-reduce(f32[]{:T(128)} %get-tuple-element.19, f32[]{:T(128)} %get-tuple-element.18), channel_id=1, replica_groups=mesh['gx'=8,'gy'=4] {'gx','gy'}, use_global_device_ids=true, to_apply=%region_13.0 | all-reduce | flops 2 | bytes 16 | tf_op jit(solution)/shard_map/psum | solution.py:79
  284.4 4.5 collective-permute-start.27
  291.2 42.5 %all-reduce.7 = (f32[]{:T(128)}, f32[]{:T(128)}) all-reduce(f32[]{:T(128)} %get-tuple-element.17, f32[]{:T(128)} %get-tuple-element.16), channel_id=1, replica_groups=mesh['gx'=8,'gy'=4] {'gx','gy'}, use_global_device_ids=true, to_apply=%region_17.0 | all-reduce | flops 2 | bytes 16 | tf_op jit(solution)/shard_map/psum | solution.py:79
  346.5 4.5 collective-permute-start.31
  353.2 41.9 %all-reduce.6 = (f32[]{:T(128)}, f32[]{:T(128)}) all-reduce(f32[]{:T(128)} %get-tuple-element.15, f32[]{:T(128)} %get-tuple-element.14), channel_id=1, replica_groups=mesh['gx'=8,'gy'=4] {'gx','gy'}, use_global_device_ids=true, to_apply=%region_21.0 | all-reduce | flops 2 | bytes 16 | tf_op jit(solution)/shard_map/psum | solution.py:79
  423.4 4.5 collective-permute-start.39
  430.0 42.7 %all-reduce.5 = (f32[]{:T(128)}, f32[]{:T(128)}) all-reduce(f32[]{:T(128)} %get-tuple-element.13, f32[]{:T(128)} %get-tuple-element.12), channel_id=1, replica_groups=mesh['gx'=8,'gy'=4] {'gx','gy'}, use_global_device_ids=true, to_apply=%region_25.0 | all-reduce | flops 2 | bytes 16 | tf_op jit(solution)/shard_map/psum | solution.py:79
  482.4 4.5 collective-permute-start.43
  489.1 42.6 %all-reduce.4 = (f32[]{:T(128)}, f32[]{:T(128)}) all-reduce(f32[]{:T(128)} %get-tuple-element.11, f32[]{:T(128)} %get-tuple-element.10), channel_id=1, replica_groups=mesh['gx'=8,'gy'=4] {'gx','gy'}, use_global_device_ids=true, to_apply=%region_29.0 | all-reduce | flops 2 | bytes 16 | tf_op jit(solution)/shard_map/psum | solution.py:79
  544.5 4.5 collective-permute-start.47
  551.2 41.8 %all-reduce.3 = (f32[]{:T(128)}, f32[]{:T(128)}) all-reduce(f32[]{:T(128)} %get-tuple-element.9, f32[]{:T(128)} %get-tuple-element.8), channel_id=1, replica_groups=mesh['gx'=8,'gy'=4] {'gx','gy'}, use_global_device_ids=true, to_apply=%region_33.0 | all-reduce | flops 2 | bytes 16 | tf_op jit(solution)/shard_map/psum | solution.py:79
  620.5 4.5 collective-permute-start.55
  627.1 42.8 %all-reduce.2 = (f32[]{:T(128)}, f32[]{:T(128)}) all-reduce(f32[]{:T(128)} %get-tuple-element.7, f32[]{:T(128)} %get-tuple-element.6), channel_id=1, replica_groups=mesh['gx'=8,'gy'=4] {'gx','gy'}, use_global_device_ids=true, to_apply=%region_37.0 | all-reduce | flops 2 | bytes 16 | tf_op jit(solution)/shard_map/psum | solution.py:79
  679.5 4.5 collective-permute-start.59
  686.3 42.5 %all-reduce.1 = (f32[]{:T(128)}, f32[]{:T(128)}) all-reduce(f32[]{:T(128)} %get-tuple-element.5, f32[]{:T(128)} %get-tuple-element.4), channel_id=1, replica_groups=mesh['gx'=8,'gy'=4] {'gx','gy'}, use_global_device_ids=true, to_apply=%region_41.0 | all-reduce | flops 2 | bytes 16 | tf_op jit(solution)/shard_map/psum | solution.py:79
  741.6 4.5 collective-permute-start.63
  748.2 41.8 %all-reduce = (f32[]{:T(128)}, f32[]{:T(128)}) all-reduce(f32[]{:T(128)} %get-tuple-element.3, f32[]{:T(128)} %get-tuple-element.2), channel_id=1, replica_groups=mesh['gx'=8,'gy'=4] {'gx','gy'}, use_global_device_ids=true, to_apply=%region_45.0 | all-reduce | flops 2 | bytes 16 | tf_op jit(solution)/shard_map/psum | solution.py:79
  (190 shorter events, 191.0 us)
Async XLA Ops:
  26.6 5.8 collective-permute-start.6
  27.9 5.9 collective-permute-start.7
  85.6 5.8 collective-permute-start.10
  86.9 5.9 collective-permute-start.11
  147.8 5.8 collective-permute-start.14
  149.1 5.9 collective-permute-start.15
  224.3 5.8 collective-permute-start.22
  225.6 5.9 collective-permute-start.23
  283.1 5.8 collective-permute-start.26
  284.4 5.9 collective-permute-start.27
  345.2 5.8 collective-permute-start.30
  346.5 5.9 collective-permute-start.31
  422.1 5.8 collective-permute-start.38
  423.4 5.9 collective-permute-start.39
  481.1 5.8 collective-permute-start.42
  482.4 5.9 collective-permute-start.43
  543.2 5.8 collective-permute-start.46
  544.5 5.9 collective-permute-start.47
  619.2 5.8 collective-permute-start.54
  620.5 5.9 collective-permute-start.55
  678.3 5.8 collective-permute-start.58
  679.5 5.9 collective-permute-start.59
  740.3 5.8 collective-permute-start.62
  741.6 5.9 collective-permute-start.63
  (45 other events, 230.0 us)
where the time goes:
time: 799 us; the launch traced here: 795 us
  blocking collectives  508 us (64%)
  starting transfers between devices  135 us (17%)
  waiting for transfers between devices  95.6 us (12%)
  between operations  40.8 us (5%)
  other arithmetic  13.3 us (2%)
    psum x12, blocking collectives, paired(): lax.psum((jnp.sum(resid * resid), jnp.sum(resid * image)), ('gx', 'gy'))  508 us
    ppermute x32, starting transfers between devices, padded_2(): lax.ppermute(tail, axis, [(i, (i + 1) % count) for i in range(ends)])  93.9 us
    ppermute x32, waiting for transfers between devices, padded_2(): lax.ppermute(head, axis, [((i + 1) % count, i) for i in range(ends)])  78.5 us
    ppermute x32, starting transfers between devices, padded_2(): lax.ppermute(head, axis, [((i + 1) % count, i) for i in range(ends)])  41.2 us
    ppermute x32, waiting for transfers between devices, padded_2(): lax.ppermute(tail, axis, [(i, (i + 1) % count) for i in range(ends)])  17.1 us
  transfers between devices with their start and end apart: 64, of which 36 were waited for; matrix products, arithmetic and copies ran while one was open for 0% of the time, Pallas kernels for 0%

commit v1 on v0

v1 whole, which is shorter than its diff:
```python
import functools

import jax
import jax.numpy as jnp
from jax import lax
from jax.experimental import pallas as pl
from jax.experimental.pallas import tpu as pltpu
from jax.sharding import PartitionSpec as P

MESH = pl.DeviceIdType.MESH

LEVELS = 2
MARGIN = 16
LANES = 128

inv_step = 0.5
coupling = 0.5

SCALE = 0.2
SHIFT = 5.5

DIRECTIONS = [(r, c) for r in (-1, 0, 1) for c in (-1, 0, 1) if (r, c) != (0, 0)]
TINY = 2e-7


def solve_small(nu):
    g00 = nu[1] / SCALE + SHIFT * nu[0]
    g01 = nu[2] / SCALE + SHIFT * nu[1]
    g02 = nu[3] / SCALE + SHIFT * nu[2]
    g12 = nu[4] / SCALE + SHIFT * nu[3]
    g22 = nu[5] / SCALE + SHIFT * nu[4]
    g11 = g02
    inv0 = 1.0 / g00
    l10 = g01 * inv0
    l20 = g02 * inv0
    d1 = g11 - l10 * g01
    ok1 = d1 > TINY * g11
    inv1 = jnp.where(ok1, 1.0 / jnp.where(ok1, d1, 1.0), 0.0)
    t = g12 - l20 * g01
    l21 = t * inv1
    d2 = g22 - l20 * g02 - l21 * t
    ok2 = ok1 & (d2 > TINY * g22)
    inv2 = jnp.where(ok2, 1.0 / jnp.where(ok2, d2, 1.0), 0.0)
    y1 = nu[1] - l10 * nu[0]
    y2 = nu[2] - l20 * nu[0] - l21 * y1
    c2 = y2 * inv2
    c1 = y1 * inv1 - l21 * c2
    c0 = nu[0] * inv0 - l10 * c1 - l20 * c2
    return c0, c1, c2


def kernel(nx, ny, term_ref, dens_ref, guess_ref, diag_ref, value_ref, out_ref,
           main, left, right, sent, slots, halo_send, halo_recv, own_sem, sum_send, sum_recv):
    rows, cols = term_ref.shape
    gx = lax.axis_index("gx")
    gy = lax.axis_index("gy")
    count = nx * ny
    me = gx * ny + gy

    barrier = pltpu.get_barrier_semaphore()

    def partner(k):
        other = lax.rem(me + k, count)
        return (other // ny, lax.rem(other, ny))

    def greet(k, carry):
        pl.semaphore_signal(barrier, inc=1, device_id=partner(k), device_id_type=MESH)
        return carry

    lax.fori_loop(1, count, greet, 0)

    here = pl.ds(MARGIN, rows)
    own = [
        pltpu.make_async_copy(term_ref, main.at[0, here], own_sem.at[0]),
        pltpu.make_async_copy(guess_ref, main.at[pl.ds(3, 2), here], own_sem.at[1]),
        pltpu.make_async_copy(diag_ref, main.at[2, here], own_sem.at[2]),
        pltpu.make_async_copy(dens_ref, main.at[1, here], own_sem.at[3]),
    ]
    for copy in own:
        copy.start()
    pl.semaphore_wait(barrier, count - 1)

    def halo(d, a):
        dr, dc = DIRECTIONS[d]
        if dr == 0:
            src_rows, dst_rows = pl.ds(0, rows), pl.ds(MARGIN, rows)
        elif dr == 1:
            src_rows, dst_rows = pl.ds(rows - MARGIN, MARGIN), pl.ds(0, MARGIN)
        else:
            src_rows, dst_rows = pl.ds(0, MARGIN), pl.ds(MARGIN + rows, MARGIN)
        if dc == 0:
            src_cols, buf = pl.ds(0, cols), main
        elif dc == 1:
            src_cols, buf = pl.ds(cols - LANES, LANES), left
        else:
            src_cols, buf = pl.ds(0, LANES), right
        if a == 1:
            src = guess_ref.at[:, src_rows, src_cols]
            dst = buf.at[pl.ds(3, 2), dst_rows, :]
        else:
            ref, at = {0: (term_ref, 0), 2: (diag_ref, 2), 3: (dens_ref, 1)}[a]
            src = ref.at[src_rows, src_cols]
            dst = buf.at[at, dst_rows, :]
        return pltpu.make_async_remote_copy(
            src_ref=src, dst_ref=dst, send_sem=halo_send.at[d, a], recv_sem=halo_recv.at[d, a],
            device_id=(gx + dr, gy + dc), device_id_type=MESH)

    def inside(dr, dc):
        ok = None
        for here_at, step, size in ((gx, dr, nx), (gy, dc, ny)):
            if step == 1:
                test = here_at < size - 1
            elif step == -1:
                test = here_at > 0
            else:
                continue
            ok = test if ok is None else ok & test
        return ok

    for d, (dr, dc) in enumerate(DIRECTIONS):
        @pl.when(inside(dr, dc))
        def _():
            for a in range(4):
                halo(d, a).start()

    for copy in own:
        copy.wait()
    for d, (dr, dc) in enumerate(DIRECTIONS):
        @pl.when(inside(-dr, -dc))
        def _():
            for a in range(4):
                halo(d, a).wait_recv()

    tall, wide = rows + 2 * MARGIN, cols + LANES
    half = LANES // 2
    lane = lax.broadcasted_iota(jnp.int32, (tall, LANES), 1)

    def field(a):
        edge = jnp.where(lane < half, right[a], left[a])
        return jnp.concatenate([main[a], edge], axis=1)

    row = lax.broadcasted_iota(jnp.int32, (tall, wide), 0)
    col = lax.broadcasted_iota(jnp.int32, (tall, wide), 1)
    row_low = jnp.where(gx > 0, 0, MARGIN)
    row_high = jnp.where(gx < nx - 1, tall, MARGIN + rows)
    col_low = jnp.where(gy < ny - 1, cols + half, cols)
    col_high = jnp.where(gy > 0, cols + half, wide)
    mask = (row >= row_low) & (row < row_high) & ((col < col_low) | (col >= col_high))

    def masked(x):
        return jnp.where(mask, x, 0.0)

    def up(x):
        return pltpu.roll(x, 1, 0)

    def down(x):
        return pltpu.roll(x, x.shape[0] - 1, 0)

    def before(x):
        return pltpu.roll(x, 1, 1)

    def after(x):
        return pltpu.roll(x, x.shape[1] - 1, 1)

    core = SCALE * (field(2) + (inv_step + 4.0 - SHIFT))

    def apply_b(v):
        beside = (up(v) + down(v)) + (before(v) + after(v))
        return core * v - SCALE * beside

    def hamiltonian(u):
        dx = u - up(u)
        dy = u - before(u)
        px, qx = jnp.maximum(dx, 0.0), jnp.minimum(dx, 0.0)
        py, qy = jnp.maximum(dy, 0.0), jnp.minimum(dy, 0.0)
        return 0.5 * ((px * px + down(qx * qx)) + (py * py + after(qy * qy)))

    def faces(u):
        sx = u - down(u)
        sy = u - after(u)
        return jnp.maximum(sx, 0.0), jnp.minimum(sx, 0.0), jnp.maximum(sy, 0.0), jnp.minimum(sy, 0.0)

    def advance(m, face):
        px, qx, py, qy = face
        fx = px * m + qx * down(m)
        fy = py * m + qy * after(m)
        return masked(inv_step * m - ((fx - up(fx)) + (fy - before(fy))))

    def mine(x):
        return x[MARGIN:MARGIN + rows, :cols]

    def dot(x, y):
        return jnp.sum(x * y, keepdims=True)

    place = lax.broadcasted_iota(jnp.int32, (1, LANES), 1)

    def reduce(which, values):
        packed = jnp.zeros((1, LANES), jnp.float32)
        for k, value in enumerate(values):
            packed = jnp.where(place == k, value, packed)
        sent[which] = packed
        slots[which, me] = packed

        def send(k, carry):
            pltpu.make_async_remote_copy(
                src_ref=sent.at[which], dst_ref=slots.at[which, me],
                send_sem=sum_send.at[which], recv_sem=sum_recv.at[which],
                device_id=partner(k), device_id_type=MESH).start()
            return carry

        lax.fori_loop(1, count, send, 0)
        others = slots.at[which, pl.ds(0, count - 1)]
        pltpu.make_async_copy(others, others, sum_recv.at[which]).wait()
        total = jnp.sum(slots[which], axis=0)
        return [total[:, k:k + 1] for k in range(len(values))]

    def basis(b):
        v1 = masked(apply_b(b))
        v2 = masked(apply_b(v1))
        v3 = apply_b(v2)
        return b, v1, v2, v3

    def pairs(x, y):
        return [dot(x[0], y[0]), dot(x[0], y[1]), dot(x[1], y[1]),
                dot(x[1], y[2]), dot(x[2], y[2]), dot(x[2], y[3])]

    later = masked(field(0))
    values = [None, None]
    for level in (1, 0):
        b = masked(inv_step * later - hamiltonian(later) + coupling * field(3 + level))
        v = basis(b)
        w = [mine(x) for x in v]
        c = solve_small(reduce(1 - level, pairs(w, w)))
        later = c[0] * v[0] + c[1] * v[1] + c[2] * v[2]
        values[level] = later
    value_ref[...] = mine(values[0])

    density = masked(field(1))
    a = basis(advance(density, faces(values[0])))
    face = faces(values[1])
    inner = [mine(x) for x in a]
    families = [[mine(x) for x in basis(advance(a[i], face))] for i in range(3)]
    moments = pairs(inner, inner)
    for i in range(3):
        for j in range(i, 3):
            moments += pairs(families[i], families[j])
    total = reduce(2, moments)
    c = solve_small(total[:6])
    nu = [0.0] * 6
    at = 6
    for i in range(3):
        for j in range(i, 3):
            weight = c[i] * c[j] * (1.0 if i == j else 2.0)
            for k in range(6):
                nu[k] = nu[k] + weight * total[at + k]
            at += 6
    e = solve_small(nu)
    result = None
    for k in range(3):
        part = c[0] * families[0][k] + c[1] * families[1][k] + c[2] * families[2][k]
        result = e[k] * part if result is None else result + e[k] * part
    out_ref[...] = result

    for d, (dr, dc) in enumerate(DIRECTIONS):
        @pl.when(inside(dr, dc))
        def _():
            for a in range(4):
                halo(d, a).wait_send()
    for which in range(3):
        others = slots.at[which, pl.ds(0, count - 1)]
        pltpu.make_async_copy(others, others, sum_send.at[which]).wait()


def solution(mesh):
    nx, ny = mesh.shape["gx"], mesh.shape["gy"]

    def shards(terminal, initial_density, density_guess, diagonal):
        rows, cols = terminal.shape
        tall = rows + 2 * MARGIN
        hbm = pl.BlockSpec(memory_space=pl.ANY)
        vmem = pl.BlockSpec(memory_space=pltpu.VMEM)
        shape = jax.ShapeDtypeStruct((rows, cols), jnp.float32)
        return pl.pallas_call(
            functools.partial(kernel, nx, ny),
            out_shape=(shape, shape),
            in_specs=[hbm] * 4,
            out_specs=(vmem, vmem),
            scratch_shapes=[
                pltpu.VMEM((5, tall, cols), jnp.float32),
                pltpu.VMEM((5, tall, LANES), jnp.float32),
                pltpu.VMEM((5, tall, LANES), jnp.float32),
                pltpu.VMEM((3, 1, LANES), jnp.float32),
                pltpu.VMEM((3, nx * ny, 1, LANES), jnp.float32),
                pltpu.SemaphoreType.DMA((8, 4)),
                pltpu.SemaphoreType.DMA((8, 4)),
                pltpu.SemaphoreType.DMA((4,)),
                pltpu.SemaphoreType.DMA((3,)),
                pltpu.SemaphoreType.DMA((3,)),
            ],
            compiler_params=pltpu.CompilerParams(collective_id=0, has_side_effects=True),
        )(terminal, initial_density, density_guess, diagonal)

    placed = (P("gx", "gy"), P("gx", "gy"), P(None, "gx", "gy"), P("gx", "gy"))
    return jax.shard_map(
        shards,
        mesh=mesh,
        in_specs=placed,
        out_specs=(P("gx", "gy"), P("gx", "gy")),
        check_vma=False,
    )
```

time: 799 us -> 36.1 us (0.05)
  blocking collectives: 508 us -> 0 us
  starting transfers between devices: 135 us -> 0 us
  waiting for transfers between devices: 95.6 us -> 0 us
  between operations: 40.8 us -> 0.65 us
  Pallas kernels: 0 us -> 33.3 us
  other arithmetic: 13.3 us -> 0 us
    psum x12 -> x0, blocking collectives: 508 us -> none  [paired(): lax.psum((jnp.sum(resid * resid), jnp.sum(resid * image)), ('gx', 'gy'))]
    ppermute x64 -> x0, starting transfers between devices: 135 us -> none  [the longest x32 93.9 us: padded_2(): lax.ppermute(tail, axis, [(i, (i + 1) % count) for i in range(ends)])]
    ppermute x64 -> x0, waiting for transfers between devices: 95.6 us -> none  [the longest x32 78.5 us: padded_2(): lax.ppermute(head, axis, [((i + 1) % count, i) for i in range(ends)])]
    pallas_call x0 -> x1, Pallas kernels: none -> 33.3 us  [shards(): pl.pallas_call(functools.partial(kernel, nx, ny), out_shape=(shape, shape...]
    reduce_sum x12 -> x0, other arithmetic: 8.75 us -> none  [paired(): jnp.sum(resid * image)]
  transfers between devices with their start and end apart: 64 -> 0, of which waited for: 36 -> 0; matrix products, arithmetic and copies ran while one was open for 0% -> 0% of each run, Pallas kernels for 0% -> 0%
where the time goes in v1:
time: 36.1 us; the launch traced here: 35.9 us
  Pallas kernels  33.3 us (92%)
  local copies, waits for them, and re-layouts  2 us (6%)
  between operations  0.65 us (2%)
    pallas_call x1, Pallas kernels, shards(): pl.pallas_call(functools.partial(kernel, nx, ny), out_shape=(shape, shape...  33.3 us
    unnamed x4, local copies, waits for them, and re-layouts  2 us

profile of v1, /device:TPU:0, one launch (start us, length us, event | category | flops | bytes accessed | tf_op | source)
XLA Modules:
  0.0 35.9 jit_solution(3636527799765244253)
XLA Ops:
  0.6 33.3 %shard_map.59 = (f32[16,512]{1,0:T(8,128)}, f32[16,512]{1,0:T(8,128)}) custom-call(f32[16,512]{1,0:T(8,128)} %term_ref.1, f32[16,512]{1,0:T(8,128)} %dens_ref.1, f32[2,16,512]{2,1,0:T(8,128)} %guess_ref.1, f32[16,512]{1,0:T(8,128)} %diag_ref.1), custom_call_target="tpu_custom_call" | custom-call | tf_op jit(solution)/shard_map/pallas_call | solution.py:283
  33.9 0.0 copy-start
  33.9 1.4 %copy.8 = f32[16,512]{1,0:T(8,128)} copy(f32[16,512]{1,0:T(8,128)} %get-tuple-element.4) | data formatting | bytes 65536
  35.3 0.0 copy-done
  35.3 0.6 %copy.9 = f32[16,512]{1,0:T(8,128)} copy(f32[16,512]{1,0:T(8,128)S(1)} %copy-done) | data formatting | bytes 65536
Async XLA Ops:
  33.9 1.4 %copy-start = (f32[16,512]{1,0:T(8,128)S(1)}, f32[16,512]{1,0:T(8,128)}, u32[]{:S(2)}) copy-start(f32[16,512]{1,0:T(8,128)} %get-tuple-element.5) | copy-start | bytes 98308

commit v2 on v1

v2 whole, which is shorter than its diff:
```python
import functools

import jax
import jax.numpy as jnp
from jax import lax
from jax.experimental import pallas as pl
from jax.experimental.pallas import tpu as pltpu
from jax.sharding import PartitionSpec as P

MESH = pl.DeviceIdType.MESH

LEVELS = 2
MARGIN = 16
LANES = 128

inv_step = 0.5
coupling = 0.5

SCALE = 0.2
SHIFT = 5.5

DIRECTIONS = [(r, c) for r in (-1, 0, 1) for c in (-1, 0, 1) if (r, c) != (0, 0)]
TINY = 2e-7


def solve_small(nu):
    g00 = nu[1] / SCALE + SHIFT * nu[0]
    g01 = nu[2] / SCALE + SHIFT * nu[1]
    g02 = nu[3] / SCALE + SHIFT * nu[2]
    g12 = nu[4] / SCALE + SHIFT * nu[3]
    g22 = nu[5] / SCALE + SHIFT * nu[4]
    g11 = g02
    inv0 = 1.0 / g00
    l10 = g01 * inv0
    l20 = g02 * inv0
    d1 = g11 - l10 * g01
    ok1 = d1 > TINY * g11
    inv1 = jnp.where(ok1, 1.0 / jnp.where(ok1, d1, 1.0), 0.0)
    t = g12 - l20 * g01
    l21 = t * inv1
    d2 = g22 - l20 * g02 - l21 * t
    ok2 = ok1 & (d2 > TINY * g22)
    inv2 = jnp.where(ok2, 1.0 / jnp.where(ok2, d2, 1.0), 0.0)
    y1 = nu[1] - l10 * nu[0]
    y2 = nu[2] - l20 * nu[0] - l21 * y1
    c2 = y2 * inv2
    c1 = y1 * inv1 - l21 * c2
    c0 = nu[0] * inv0 - l10 * c1 - l20 * c2
    return c0, c1, c2


def kernel(nx, ny, term_ref, dens_ref, guess_ref, diag_ref, value_ref, out_ref,
           main, left, right, sent, slots, halo_send, halo_recv, own_sem, sum_send, sum_recv,
           ready):
    rows, cols = term_ref.shape
    gx = lax.axis_index("gx")
    gy = lax.axis_index("gy")
    count = nx * ny
    me = gx * ny + gy

    def inside(dr, dc):
        ok = None
        for here_at, step, size in ((gx, dr, nx), (gy, dc, ny)):
            if step == 1:
                test = here_at < size - 1
            elif step == -1:
                test = here_at > 0
            else:
                continue
            ok = test if ok is None else ok & test
        return ok

    def across(k):
        return (lax.rem(gx + k, nx), gy)

    def along(k):
        return (gx, lax.rem(gy + k, ny))

    barrier = pltpu.get_barrier_semaphore()
    greeted = nx + ny - 2
    for k in range(1, nx):
        pl.semaphore_signal(barrier, inc=1, device_id=across(k), device_id_type=MESH)
    for k in range(1, ny):
        pl.semaphore_signal(barrier, inc=1, device_id=along(k), device_id_type=MESH)
    for dr, dc in DIRECTIONS:
        if dr != 0 and dc != 0:
            there = inside(dr, dc)
            greeted = greeted + jnp.where(there, 1, 0)

            @pl.when(there)
            def _():
                pl.semaphore_signal(
                    barrier, inc=1, device_id=(gx + dr, gy + dc), device_id_type=MESH)

    here = pl.ds(MARGIN, rows)
    own = [
        pltpu.make_async_copy(source, main.at[at, here], own_sem.at[at])
        for at, source in enumerate(
            (term_ref, diag_ref, guess_ref.at[1], guess_ref.at[0], dens_ref))
    ]
    for copy in own:
        copy.start()
    for copy in own:
        copy.wait()
    pl.semaphore_wait(barrier, greeted)

    def pieces(dr):
        if dr == 0:
            return [(0, 3, 0, rows), (3, 2, 0, rows)]
        return [(0, 3, 0, 8), (0, 4, 8, 8), (3, 2, 0, 8)]

    def halo(d, piece):
        dr, dc = DIRECTIONS[d]
        first, many, out, size = pieces(dr)[piece]
        if dr == 0:
            src_rows, dst_rows = here, here
        elif dr == 1:
            src_rows = pl.ds(MARGIN + rows - out - size, size)
            dst_rows = pl.ds(MARGIN - out - size, size)
        else:
            src_rows = pl.ds(MARGIN + out, size)
            dst_rows = pl.ds(MARGIN + rows + out, size)
        if dc == 0:
            src_cols, buf = pl.ds(0, cols), main
        elif dc == 1:
            src_cols, buf = pl.ds(cols - LANES, LANES), left
        else:
            src_cols, buf = pl.ds(0, LANES), right
        return pltpu.make_async_remote_copy(
            src_ref=main.at[pl.ds(first, many), src_rows, src_cols],
            dst_ref=buf.at[pl.ds(first, many), dst_rows, :],
            send_sem=halo_send.at[d, piece], recv_sem=halo_recv.at[d, piece],
            device_id=(gx + dr, gy + dc), device_id_type=MESH)

    def each_halo(near, act, back=False):
        for d, (dr, dc) in enumerate(DIRECTIONS):
            @pl.when(inside(-dr, -dc) if back else inside(dr, dc))
            def _():
                for piece in [0] if near else range(1, len(pieces(dr))):
                    act(halo(d, piece))

    each_halo(True, lambda copy: copy.start())
    for k in range(1, nx):
        pl.semaphore_signal(ready, inc=1, device_id=across(k), device_id_type=MESH)
    each_halo(False, lambda copy: copy.start())

    wide = cols + LANES
    half = LANES // 2
    tall = rows + 2 * MARGIN
    low_mid, high_mid = MARGIN - 8, MARGIN + rows + 8

    def mask_of(size, cyclic, margin):
        row = lax.broadcasted_iota(jnp.int32, (size, wide), 0)
        col = lax.broadcasted_iota(jnp.int32, (size, wide), 1)
        col_low = jnp.where(gy < ny - 1, cols + half, cols)
        col_high = jnp.where(gy > 0, cols + half, wide)
        ok = (col < col_low) | (col >= col_high)
        if cyclic:
            row_low = jnp.where(gx < nx - 1, rows + 4, rows)
            row_high = jnp.where(gx > 0, rows + 4, size)
            return ok & ((row < row_low) | (row >= row_high))
        row_low = jnp.where(gx > 0, 0, margin)
        row_high = jnp.where(gx < nx - 1, size, margin + rows)
        return ok & (row >= row_low) & (row < row_high)

    masks = {
        "tall": mask_of(tall, False, MARGIN),
        "mid": mask_of(rows + 16, False, 8),
        "small": mask_of(rows + 8, True, 4),
    }

    def shrink(x, start):
        sub = lax.broadcasted_iota(jnp.int32, (8, x.shape[1]), 0)
        ends = jnp.where(sub < 4, x[start + rows:start + rows + 8], x[start - 8:start])
        return jnp.concatenate([x[start:start + rows], ends], axis=0)

    def strip(a, begin, end):
        lane = lax.broadcasted_iota(jnp.int32, (end - begin, LANES), 1)
        edge = jnp.where(lane < half, right[a, begin:end], left[a, begin:end])
        return jnp.concatenate([main[a, begin:end], edge], axis=1)

    def field(a, window):
        if window == "tall":
            return strip(a, 0, tall)
        x = strip(a, low_mid, high_mid)
        return x if window == "mid" else shrink(x, 8)

    def up(x):
        return pltpu.roll(x, 1, 0)

    def down(x):
        return pltpu.roll(x, x.shape[0] - 1, 0)

    def before(x):
        return pltpu.roll(x, 1, 1)

    def after(x):
        return pltpu.roll(x, x.shape[1] - 1, 1)

    def masked(x, window):
        return jnp.where(masks[window], x, 0.0)

    def core_of(window):
        return SCALE * (field(1, window) + (inv_step + 4.0 - SHIFT))

    def apply_b(v, core):
        beside = (up(v) + down(v)) + (before(v) + after(v))
        return core * v - SCALE * beside

    def hamiltonian(u):
        dx = u - up(u)
        dy = u - before(u)
        px, qx = jnp.maximum(dx, 0.0), jnp.minimum(dx, 0.0)
        py, qy = jnp.maximum(dy, 0.0), jnp.minimum(dy, 0.0)
        return 0.5 * ((px * px + down(qx * qx)) + (py * py + after(qy * qy)))

    def faces(u):
        sx = u - down(u)
        sy = u - after(u)
        return jnp.maximum(sx, 0.0), jnp.minimum(sx, 0.0), jnp.maximum(sy, 0.0), jnp.minimum(sy, 0.0)

    def advance(m, face, window):
        px, qx, py, qy = face
        fx = px * m + qx * down(m)
        fy = py * m + qy * after(m)
        return masked(inv_step * m - ((fx - up(fx)) + (fy - before(fy))), window)

    def value_rhs(later, level, window):
        return masked(inv_step * later - hamiltonian(later)
                      + coupling * field(2 if level == 1 else 3, window), window)

    def dot(x, y):
        return jnp.sum(x * y, keepdims=True)

    place = lax.broadcasted_iota(jnp.int32, (1, LANES), 1)

    def send_sums(which, values):
        packed = jnp.zeros((1, LANES), jnp.float32)
        for k, value in enumerate(values):
            packed = jnp.where(place == k, value, packed)
        sent[which] = packed
        slots[which, me] = packed

        def send(px, py):
            pltpu.make_async_remote_copy(
                src_ref=sent.at[which], dst_ref=slots.at[which, me],
                send_sem=sum_send.at[which], recv_sem=sum_recv.at[which],
                device_id=(px, py), device_id_type=MESH).start()

        columns = [lax.rem(gy + k, ny) for k in range(ny)]

        def line(k, carry):
            px = lax.rem(gx + k, nx)
            for py in columns:
                send(px, py)
            return carry

        lax.fori_loop(1, nx, line, 0)
        for py in columns[1:]:
            send(gx, py)

    def take_sums(which, many):
        others = slots.at[which, pl.ds(0, count - 1)]
        pltpu.make_async_copy(others, others, sum_recv.at[which]).wait()
        total = jnp.sum(slots[which], axis=0)
        return [total[:, k:k + 1] for k in range(many)]

    def basis(b, core, window, last=True):
        v1 = masked(apply_b(b, core), window)
        v2 = masked(apply_b(v1, core), window)
        return (b, v1, v2, apply_b(v2, core)) if last else (b, v1, v2)

    def mix(c, v):
        return c[0] * v[0] + c[1] * v[1] + c[2] * v[2]

    def pairs(x, y):
        return [dot(x[0], y[0]), dot(x[0], y[1]), dot(x[1], y[1]),
                dot(x[1], y[2]), dot(x[2], y[2]), dot(x[2], y[3])]

    def own_small(v):
        return [x[:rows, :cols] for x in v]

    each_halo(True, lambda copy: copy.wait_recv(), back=True)
    small_core = core_of("small")
    later = masked(field(0, "small"), "small")
    w = own_small(basis(value_rhs(later, 1, "small"), small_core, "small"))
    moments = pairs(w, w)
    pl.semaphore_wait(ready, nx - 1)
    send_sums(0, moments)
    each_halo(False, lambda copy: copy.wait_recv(), back=True)
    core = core_of("tall")
    later = masked(field(0, "tall"), "tall")
    v = basis(value_rhs(later, 1, "tall"), core, "tall", last=False)
    vs = [shrink(x, MARGIN) for x in v]
    c = solve_small(take_sums(0, 6))

    first_small = mix(c, vs)
    w = own_small(basis(value_rhs(first_small, 0, "small"), small_core, "small"))
    send_sums(1, pairs(w, w))
    first = mix(c, v)
    v = basis(value_rhs(first, 0, "tall"), core, "tall", last=False)
    v = [x[low_mid:high_mid] for x in v]
    face = faces(first_small)
    density = masked(field(4, "mid"), "mid")
    mid_core = core_of("mid")
    c = solve_small(take_sums(1, 6))
    second = mix(c, v)

    a = basis(advance(density, faces(second), "mid"), mid_core, "mid", last=False)
    a = [shrink(x, 8) for x in a]
    last = apply_b(a[2], small_core)
    inner = own_small(a + [last])
    families = [
        own_small(basis(advance(a[i], face, "small"), small_core, "small")) for i in range(3)]
    moments = pairs(inner, inner)
    for i in range(3):
        for j in range(i, 3):
            moments += pairs(families[i], families[j])
    send_sums(2, moments)
    value_ref[...] = second[8:8 + rows, :cols]
    total = take_sums(2, len(moments))
    c = solve_small(total[:6])
    nu = [0.0] * 6
    at = 6
    for i in range(3):
        for j in range(i, 3):
            weight = c[i] * c[j] * (1.0 if i == j else 2.0)
            for k in range(6):
                nu[k] = nu[k] + weight * total[at + k]
            at += 6
    e = solve_small(nu)
    result = None
    for i in range(3):
        for k in range(3):
            part = (c[i] * e[k]) * families[i][k]
            result = part if result is None else result + part
    out_ref[...] = result

    each_halo(True, lambda copy: copy.wait_send())
    each_halo(False, lambda copy: copy.wait_send())
    for which in range(3):
        others = slots.at[which, pl.ds(0, count - 1)]
        pltpu.make_async_copy(others, others, sum_send.at[which]).wait()


def deliver(value_ref, density_ref, value_out, density_out):
    value_out[...] = value_ref[...]
    density_out[...] = density_ref[...]


def solution(mesh):
    nx, ny = mesh.shape["gx"], mesh.shape["gy"]

    def shards(terminal, initial_density, density_guess, diagonal):
        rows, cols = terminal.shape
        tall = rows + 2 * MARGIN
        hbm = pl.BlockSpec(memory_space=pl.ANY)
        vmem = pl.BlockSpec(memory_space=pltpu.VMEM)
        shape = jax.ShapeDtypeStruct((rows, cols), jnp.float32)
        value, density = pl.pallas_call(
            functools.partial(kernel, nx, ny),
            out_shape=(shape, shape),
            in_specs=[hbm] * 4,
            out_specs=(vmem, vmem),
            scratch_shapes=[
                pltpu.VMEM((5, tall, cols), jnp.float32),
                pltpu.VMEM((5, tall, LANES), jnp.float32),
                pltpu.VMEM((5, tall, LANES), jnp.float32),
                pltpu.VMEM((3, 1, LANES), jnp.float32),
                pltpu.VMEM((3, nx * ny, 1, LANES), jnp.float32),
                pltpu.SemaphoreType.DMA((8, 3)),
                pltpu.SemaphoreType.DMA((8, 3)),
                pltpu.SemaphoreType.DMA((5,)),
                pltpu.SemaphoreType.DMA((3,)),
                pltpu.SemaphoreType.DMA((3,)),
                pltpu.SemaphoreType.REGULAR,
            ],
            compiler_params=pltpu.CompilerParams(collective_id=0, has_side_effects=True),
        )(terminal, initial_density, density_guess, diagonal)
        return pl.pallas_call(
            deliver,
            out_shape=(shape, shape),
            in_specs=[vmem] * 2,
            out_specs=(vmem, vmem),
        )(value, density)

    placed = (P("gx", "gy"), P("gx", "gy"), P(None, "gx", "gy"), P("gx", "gy"))
    return jax.shard_map(
        shards,
        mesh=mesh,
        in_specs=placed,
        out_specs=(P("gx", "gy"), P("gx", "gy")),
        check_vma=False,
    )
```

time: 36.1 us -> 31.6 us (0.88)
  Pallas kernels: 33.3 us -> 30.7 us
  local copies, waits for them, and re-layouts: 2 us -> 0 us
    pallas_call x1, Pallas kernels: 33.3 us -> 29.3 us  [shards(): pl.pallas_call(functools.partial(kernel, nx, ny), out_shape=(shape, shape...]
    unnamed x4 -> x0, local copies, waits for them, and re-layouts: 2 us -> none
    pallas_call x0 -> x1, Pallas kernels: none -> 1.4 us  [shards(): pl.pallas_call(deliver, out_shape=(shape, shape), in_specs=[vmem] * 2, ou...]
where the time goes in v2:
time: 31.6 us; the launch traced here: 31.4 us
  Pallas kernels  30.7 us (97%)
  between operations  0.64 us (2%)
    pallas_call x1, Pallas kernels, shards(): pl.pallas_call(functools.partial(kernel, nx, ny), out_shape=(shape, shape...  29.3 us
    pallas_call x1, Pallas kernels, shards(): pl.pallas_call(deliver, out_shape=(shape, shape), in_specs=[vmem] * 2, ou...  1.4 us

profile of v2, /device:TPU:0, one launch (start us, length us, event | category | flops | bytes accessed | tf_op | source)
XLA Modules:
  0.0 31.4 jit_solution(6687896849391205897)
XLA Ops:
  0.6 29.3 %shard_map.59 = (f32[16,512]{1,0:T(8,128)}, f32[16,512]{1,0:T(8,128)}) custom-call(f32[16,512]{1,0:T(8,128)} %term_ref.1, f32[16,512]{1,0:T(8,128)} %dens_ref.1, f32[2,16,512]{2,1,0:T(8,128)} %guess_ref.1, f32[16,512]{1,0:T(8,128)} %diag_ref.1), custom_call_target="tpu_custom_call" | custom-call | tf_op jit(solution)/shard_map/pallas_call | solution.py:360
  30.0 1.4 %shard_map.60 = (f32[16,512]{1,0:T(8,128)}, f32[16,512]{1,0:T(8,128)}) custom-call(f32[16,512]{1,0:T(8,128)} %get-tuple-element.4.value_ref, f32[16,512]{1,0:T(8,128)} %get-tuple-element.5.density_ref), custom_call_target="tpu_custom_call" | custom-call | tf_op jit(solution)/shard_map/pallas_call | solution.py:380

commit v3 on v2

--- a/solution.py
+++ b/solution.py
@@ -16,7 +16,7 @@
 inv_step = 0.5
 coupling = 0.5
 
-SCALE = 0.2
+SCALE = 0.25
 SHIFT = 5.5
 
 DIRECTIONS = [(r, c) for r in (-1, 0, 1) for c in (-1, 0, 1) if (r, c) != (0, 0)]
@@ -49,9 +49,9 @@
     return c0, c1, c2
 
 
-def kernel(nx, ny, term_ref, dens_ref, guess_ref, diag_ref, value_ref, out_ref,
+def kernel(nx, ny, term_ref, dens_ref, guess_ref, diag_ref, both_ref,
            main, left, right, sent, slots, halo_send, halo_recv, own_sem, sum_send, sum_recv,
-           ready):
+           ready, scaled_tall, scaled_mid, scaled_small):
     rows, cols = term_ref.shape
     gx = lax.axis_index("gx")
     gy = lax.axis_index("gy")
@@ -100,6 +100,30 @@
     ]
     for copy in own:
         copy.start()
+    wide = cols + LANES
+    half = LANES // 2
+    tall = rows + 2 * MARGIN
+    low_mid, high_mid = MARGIN - 8, MARGIN + rows + 8
+
+    def mask_of(size, cyclic, margin):
+        row = lax.broadcasted_iota(jnp.int32, (size, wide), 0)
+        col = lax.broadcasted_iota(jnp.int32, (size, wide), 1)
+        col_low = jnp.where(gy < ny - 1, cols + half, cols)
+        col_high = jnp.where(gy > 0, cols + half, wide)
+        ok = (col < col_low) | (col >= col_high)
+        if cyclic:
+            row_low = jnp.where(gx < nx - 1, rows + 4, rows)
+            row_high = jnp.where(gx > 0, rows + 4, size)
+            return ok & ((row < row_low) | (row >= row_high))
+        row_low = jnp.where(gx > 0, 0, margin)
+        row_high = jnp.where(gx < nx - 1, size, margin + rows)
+        return ok & (row >= row_low) & (row < row_high)
+
+    scaled = {"tall": scaled_tall, "mid": scaled_mid, "small": scaled_small}
+    scaled_tall[...] = jnp.where(mask_of(tall, False, MARGIN), SCALE, 0.0)
+    scaled_mid[...] = jnp.where(mask_of(rows + 16, False, 8), SCALE, 0.0)
+    scaled_small[...] = jnp.where(mask_of(rows + 8, True, 4), SCALE, 0.0)
+
     for copy in own:
         copy.wait()
     pl.semaphore_wait(barrier, greeted)
@@ -144,31 +168,6 @@
         pl.semaphore_signal(ready, inc=1, device_id=across(k), device_id_type=MESH)
     each_halo(False, lambda copy: copy.start())
 
-    wide = cols + LANES
-    half = LANES // 2
-    tall = rows + 2 * MARGIN
-    low_mid, high_mid = MARGIN - 8, MARGIN + rows + 8
-
-    def mask_of(size, cyclic, margin):
-        row = lax.broadcasted_iota(jnp.int32, (size, wide), 0)
-        col = lax.broadcasted_iota(jnp.int32, (size, wide), 1)
-        col_low = jnp.where(gy < ny - 1, cols + half, cols)
-        col_high = jnp.where(gy > 0, cols + half, wide)
-        ok = (col < col_low) | (col >= col_high)
-        if cyclic:
-            row_low = jnp.where(gx < nx - 1, rows + 4, rows)
-            row_high = jnp.where(gx > 0, rows + 4, size)
-            return ok & ((row < row_low) | (row >= row_high))
-        row_low = jnp.where(gx > 0, 0, margin)
-        row_high = jnp.where(gx < nx - 1, size, margin + rows)
-        return ok & (row >= row_low) & (row < row_high)
-
-    masks = {
-        "tall": mask_of(tall, False, MARGIN),
-        "mid": mask_of(rows + 16, False, 8),
-        "small": mask_of(rows + 8, True, 4),
-    }
-
     def shrink(x, start):
         sub = lax.broadcasted_iota(jnp.int32, (8, x.shape[1]), 0)
         ends = jnp.where(sub < 4, x[start + rows:start + rows + 8], x[start - 8:start])
@@ -198,21 +197,24 @@
         return pltpu.roll(x, x.shape[1] - 1, 1)
 
     def masked(x, window):
-        return jnp.where(masks[window], x, 0.0)
+        return jnp.where(scaled[window][...] > 0.0, x, 0.0)
 
     def core_of(window):
-        return SCALE * (field(1, window) + (inv_step + 4.0 - SHIFT))
-
-    def apply_b(v, core):
+        return masked(SCALE * (field(1, window) + (inv_step + 4.0 - SHIFT)), window)
+
+    def apply_b(v, core, window):
         beside = (up(v) + down(v)) + (before(v) + after(v))
-        return core * v - SCALE * beside
+        return core * v - scaled[window][...] * beside
+
+    def apply_half(v, core):
+        return (0.5 * core) * v - SCALE * (down(v) + after(v))
 
     def hamiltonian(u):
         dx = u - up(u)
         dy = u - before(u)
         px, qx = jnp.maximum(dx, 0.0), jnp.minimum(dx, 0.0)
         py, qy = jnp.maximum(dy, 0.0), jnp.minimum(dy, 0.0)
-        return 0.5 * ((px * px + down(qx * qx)) + (py * py + after(qy * qy)))
+        return (px * px + down(qx * qx)) + (py * py + after(qy * qy))
 
     def faces(u):
         sx = u - down(u)
@@ -223,21 +225,45 @@
         px, qx, py, qy = face
         fx = px * m + qx * down(m)
         fy = py * m + qy * after(m)
-        return masked(inv_step * m - ((fx - up(fx)) + (fy - before(fy))), window)
+        net = (fx - up(fx)) + (fy - before(fy))
+        return scaled[window][...] * ((inv_step / SCALE) * m - (1.0 / SCALE) * net)
 
     def value_rhs(later, level, window):
-        return masked(inv_step * later - hamiltonian(later)
-                      + coupling * field(2 if level == 1 else 3, window), window)
+        guess = masked(coupling * field(2 if level == 1 else 3, window), window)
+        own_part = (inv_step / SCALE) * later - (0.5 / SCALE) * hamiltonian(later)
+        return scaled[window][...] * own_part + guess
+
+    def fold(p):
+        parts = [p[i:i + 8, j:j + LANES] for i in range(0, rows, 8) for j in range(0, cols, LANES)]
+        while len(parts) > 1:
+            odd = parts[len(parts) // 2 * 2:]
+            parts = [parts[i] + parts[i + 1] for i in range(0, len(parts) - 1, 2)] + odd
+        return parts[0]
 
     def dot(x, y):
-        return jnp.sum(x * y, keepdims=True)
-
-    place = lax.broadcasted_iota(jnp.int32, (1, LANES), 1)
+        return fold(x * y)
+
+    sub8 = lax.broadcasted_iota(jnp.int32, (8, LANES), 0)
+    lane8 = lax.broadcasted_iota(jnp.int32, (8, LANES), 1)
+
+    def pack(tiles):
+        spread = None
+        for first in range(0, len(tiles), 8):
+            group = tiles[first:first + 8]
+            group = group + [jnp.zeros((8, LANES), jnp.float32)] * (8 - len(group))
+            for step in (4, 2, 1):
+                keep = lax.rem(sub8, 2 * step) < step
+                group = [
+                    jnp.where(keep, a + pltpu.roll(a, 8 - step, 0), b + pltpu.roll(b, step, 0))
+                    for a, b in zip(group[:step], group[step:])
+                ]
+            sums = jnp.sum(group[0], axis=1, keepdims=True)
+            part = jnp.where(lane8 == sub8 + first, sums, 0.0)
+            spread = part if spread is None else spread + part
+        return jnp.sum(spread, axis=0, keepdims=True)
 
     def send_sums(which, values):
-        packed = jnp.zeros((1, LANES), jnp.float32)
-        for k, value in enumerate(values):
-            packed = jnp.where(place == k, value, packed)
+        packed = pack(values)
         sent[which] = packed
         slots[which, me] = packed
 
@@ -266,16 +292,18 @@
         return [total[:, k:k + 1] for k in range(many)]
 
     def basis(b, core, window, last=True):
-        v1 = masked(apply_b(b, core), window)
-        v2 = masked(apply_b(v1, core), window)
-        return (b, v1, v2, apply_b(v2, core)) if last else (b, v1, v2)
+        v1 = apply_b(b, core, window)
+        v2 = apply_b(v1, core, window)
+        return (b, v1, v2, apply_half(v2, core)) if last else (b, v1, v2)
 
     def mix(c, v):
         return c[0] * v[0] + c[1] * v[1] + c[2] * v[2]
 
     def pairs(x, y):
         return [dot(x[0], y[0]), dot(x[0], y[1]), dot(x[1], y[1]),
-                dot(x[1], y[2]), dot(x[2], y[2]), dot(x[2], y[3])]
+                dot(x[1], y[2]), dot(x[2], y[2]),
+                2.0 * dot(x[2], x[3]) if x is y
+                else fold(x[2] * y[3] + y[2] * x[3])]
 
     def own_small(v):
         return [x[:rows, :cols] for x in v]
@@ -308,7 +336,7 @@
 
     a = basis(advance(density, faces(second), "mid"), mid_core, "mid", last=False)
     a = [shrink(x, 8) for x in a]
-    last = apply_b(a[2], small_core)
+    last = apply_half(a[2], small_core)
     inner = own_small(a + [last])
     families = [
         own_small(basis(advance(a[i], face, "small"), small_core, "small")) for i in range(3)]
@@ -317,7 +345,12 @@
         for j in range(i, 3):
             moments += pairs(families[i], families[j])
     send_sums(2, moments)
-    value_ref[...] = second[8:8 + rows, :cols]
+    both_ref[0] = second[8:8 + rows, :cols]
+    each_halo(True, lambda copy: copy.wait_send())
+    each_halo(False, lambda copy: copy.wait_send())
+    for which in range(3):
+        others = slots.at[which, pl.ds(0, count - 1)]
+        pltpu.make_async_copy(others, others, sum_send.at[which]).wait()
     total = take_sums(2, len(moments))
     c = solve_small(total[:6])
     nu = [0.0] * 6
@@ -334,18 +367,7 @@
         for k in range(3):
             part = (c[i] * e[k]) * families[i][k]
             result = part if result is None else result + part
-    out_ref[...] = result
-
-    each_halo(True, lambda copy: copy.wait_send())
-    each_halo(False, lambda copy: copy.wait_send())
-    for which in range(3):
-        others = slots.at[which, pl.ds(0, count - 1)]
-        pltpu.make_async_copy(others, others, sum_send.at[which]).wait()
-
-
-def deliver(value_ref, density_ref, value_out, density_out):
-    value_out[...] = value_ref[...]
-    density_out[...] = density_ref[...]
+    both_ref[1] = result
 
 
 def solution(mesh):
@@ -357,11 +379,11 @@
         hbm = pl.BlockSpec(memory_space=pl.ANY)
         vmem = pl.BlockSpec(memory_space=pltpu.VMEM)
         shape = jax.ShapeDtypeStruct((rows, cols), jnp.float32)
-        value, density = pl.pallas_call(
+        both = pl.pallas_call(
             functools.partial(kernel, nx, ny),
-            out_shape=(shape, shape),
+            out_shape=jax.ShapeDtypeStruct((2, rows, cols), jnp.float32),
             in_specs=[hbm] * 4,
-            out_specs=(vmem, vmem),
+            out_specs=vmem,
             scratch_shapes=[
                 pltpu.VMEM((5, tall, cols), jnp.float32),
                 pltpu.VMEM((5, tall, LANES), jnp.float32),
@@ -374,15 +396,13 @@
                 pltpu.SemaphoreType.DMA((3,)),
                 pltpu.SemaphoreType.DMA((3,)),
                 pltpu.SemaphoreType.REGULAR,
+                pltpu.VMEM((tall, cols + LANES), jnp.float32),
+                pltpu.VMEM((rows + 16, cols + LANES), jnp.float32),
+                pltpu.VMEM((rows + 8, cols + LANES), jnp.float32),
             ],
             compiler_params=pltpu.CompilerParams(collective_id=0, has_side_effects=True),
         )(terminal, initial_density, density_guess, diagonal)
-        return pl.pallas_call(
-            deliver,
-            out_shape=(shape, shape),
-            in_specs=[vmem] * 2,
-            out_specs=(vmem, vmem),
-        )(value, density)
+        return both[0], both[1]
 
     placed = (P("gx", "gy"), P("gx", "gy"), P(None, "gx", "gy"), P("gx", "gy"))
     return jax.shard_map(

time: 31.6 us -> 31.4 us (level)
  Pallas kernels: 30.7 us -> 29.1 us
  local copies, waits for them, and re-layouts: 0 us -> 1.41 us
    pallas_call x2 -> x1, Pallas kernels: 30.7 us -> 29.1 us  [shards(): pl.pallas_call(functools.partial(kernel, nx, ny), out_shape=jax.ShapeDtyp...]
    squeeze x0 -> x1, local copies, waits for them, and re-layouts: none -> 1.41 us  [shards(): return (both[0], both[1])]
where the time goes in v3:
time: 31.4 us; the launch traced here: 31.1 us
  Pallas kernels  29.1 us (93%)
  local copies, waits for them, and re-layouts  1.41 us (4%)
  between operations  0.64 us (2%)
    pallas_call x1, Pallas kernels, shards(): pl.pallas_call(functools.partial(kernel, nx, ny), out_shape=jax.ShapeDtyp...  29.1 us
    squeeze x1, local copies, waits for them, and re-layouts, shards(): return (both[0], both[1])  1.41 us

profile of v3, /device:TPU:0, one launch (start us, length us, event | category | flops | bytes accessed | tf_op | source)
XLA Modules:
  0.0 31.1 jit_solution(4191677057845004744)
XLA Ops:
  0.6 29.1 %shard_map.59 = f32[2,16,512]{2,1,0:T(8,128)} custom-call(f32[16,512]{1,0:T(8,128)} %term_ref.1, f32[16,512]{1,0:T(8,128)} %dens_ref.1, f32[2,16,512]{2,1,0:T(8,128)} %guess_ref.1, f32[16,512]{1,0:T(8,128)} %diag_ref.1), custom_call_target="tpu_custom_call" | custom-call | tf_op jit(solution)/shard_map/pallas_call | solution.py:382
  29.7 1.4 %slice_bitcast_fusion = (f32[16,512]{1,0:T(8,128)}, f32[16,512]{1,0:T(8,128)}) fusion(f32[2,16,512]{2,1,0:T(8,128)} %shard_map.59), kind=kLoop, calls=%fused_computation | loop fusion | bytes 131072 | tf_op jit(solution)/shard_map/squeeze | solution.py:405
